TPU v7x, 32 devices: a whole 2x2x4 slice. The times are simulated.
32 devices in a mesh: grp: 2 (over y), col: 4 (over z), slc: 2 (over x), bat: 2 (over core).
Axes of the slice: x: 2, y: 2, z: 4, core: 2. Of those that a mesh axis runs over, the one named last changes fastest.
Arguments:
- site_tensors: bfloat16 [4, 72, 2, 64, 128], P(('grp', 'slc'), 'col'), parts along dimension 0, may hold values from -1.2 to 1.2
- left_edge: float32 [4, 64, 128], P(('grp', 'slc')), parts along dimension 0, may hold values from -0.5 to 0.5
- right_edge: float32 [4, 64, 128], P(('grp', 'slc')), parts along dimension 0, may hold values from -0.5 to 0.5
- order: int32 [144], P(('grp', 'col')), parts along dimension 0, may hold values from 0 to 71, each once
- bitstrings: int32 [128, 72], P(('grp', 'bat')), parts along dimension 0, may hold values 0 or 1
Outputs:
- amplitudes: float32 [2, 128], P(None, ('grp', 'bat')), parts along dimension 1
There are 2 independent parts, one for each index of `grp`. A program takes and returns all parts, laid end to end along the dimension named above; each array names one. Nothing has to cross between parts.
Inputs may be any that keep to these rules, and one draw needn't show every extreme that they name: `order`: a permutation of the 72 qubit indices.
All inputs are finite; a program needn't handle non-finite values. No bound on the sum of `bitstrings` on one device may be relied on, other than what follows from the above.
Results may differ from a plain program's by a relative error of at most 0.0003.
Values sent between devices are 32-bit elements; how exact they have to be, the bound alone decides.
A program may use at most 64 MiB of HBM per device.

v0:
```python
import jax
import jax.numpy as jnp
from jax import lax
from jax.sharding import PartitionSpec as P


def rotate(block):
    middle = block.shape[-1] // 2
    return jnp.concatenate([-block[..., middle:], block[..., :middle]], axis=-1)


def complex_product(first_factor, second_factor):
    stacked = jnp.concatenate([second_factor, rotate(second_factor)], axis=-2)
    return jnp.einsum("bij,bjk->bik", first_factor, stacked, precision=lax.Precision.HIGHEST)


def closing(boundary, edge):
    middle = boundary.shape[-1] // 2
    real_left = boundary[..., :middle]
    imag_left = boundary[..., middle:]
    real_right = edge[..., :middle]
    imag_right = edge[..., middle:]
    real_part = jnp.sum(real_left * real_right - imag_left * imag_right, axis=(1, 2))
    imag_part = jnp.sum(real_left * imag_right + imag_left * real_right, axis=(1, 2))
    return jnp.stack([real_part, imag_part])


def select_site(tensors, site_bits, position):
    matrices = lax.dynamic_index_in_dim(tensors, position, 0, keepdims=False)
    chosen_bits = lax.dynamic_index_in_dim(site_bits, position, 1, keepdims=False)
    return jnp.where(chosen_bits[:, None, None] == 1, matrices[1], matrices[0])


def column_product(tensors, site_bits):
    site_count = tensors.shape[0]
    leading = select_site(tensors, site_bits, 0)
    return lax.fori_loop(
        1,
        site_count,
        lambda position, carried: complex_product(
            carried, select_site(tensors, site_bits, position)
        ),
        leading,
    )


def on_device(site_tensors, left_edge, right_edge, order, bitstrings):
    col_count = lax.axis_size("col")
    col_index = lax.axis_index("col")
    tensors = site_tensors[0].astype(jnp.float32)
    site_bits = jnp.take(bitstrings, order, axis=1)
    batch_rows = site_bits.shape[0]
    bond_size = left_edge.shape[1]
    product = column_product(tensors, site_bits)
    share = (batch_rows + col_count - 1) // col_count
    padded_rows = share * col_count
    grouped = product.reshape(col_count, share, bond_size, 2 * bond_size)
    received = lax.all_to_all(grouped, "col", split_axis=0, concat_axis=0, tiled=True)
    items = received.shape[1]
    start = jnp.broadcast_to(left_edge[0], (items, bond_size, 2 * bond_size))
    final_state = lax.fori_loop(
        0,
        received.shape[0],
        lambda position, carried: complex_product(
            carried, lax.dynamic_index_in_dim(received, position, 0, keepdims=False)
        ),
        start,
    )
    closed = closing(final_state, right_edge[0])
    placed = lax.dynamic_update_slice(
        jnp.zeros((2, padded_rows), jnp.float32), closed, (jnp.int32(0), col_index * share)
    )
    return lax.psum(placed, ("col", "slc"))


def solution(mesh):
    return jax.shard_map(
        on_device,
        mesh=mesh,
        in_specs=(
            P(("grp", "slc"), "col", None, None, None),
            P(("grp", "slc"), None, None),
            P(("grp", "slc"), None, None),
            P(("grp", "col")),
            P(("grp", "bat"), None),
        ),
        out_specs=P(None, ("grp", "bat")),
        check_vma=False,
    )
```

profile of v0, /device:TPU:0, one launch (start us, length us, event | category | flops | bytes accessed | tf_op | source)
XLA Modules:
  0.0 143.9 jit_solution(12536998118196753343)
XLA Ops:
  0.0 0.7 compare_select_fusion
  0.7 0.7 compare_and_fusion
  1.3 1.2 bitcast_convert_fusion
  2.6 0.6 gather_fusion
  3.3 1.1 broadcast_select_fusion.1
  4.4 83.2 %while.28 = (s32[]{:T(128)}, f32[32,64,128]{2,1,0:T(8,128)}, s32[32,18]{0,1:T(8,128)S(1)}, f32[18,2,64,128]{3,2,1,0:T(8,128)S(1)}, s32[]{:T(128)}, /*index=5*/s32[]{:T(128)}, s32[]{:T(128)}, s32[]{}) while((s32[]{:T(128)}, f32[32,64,128]{2,1,0:T(8,128)}, s32[32,18]{0,1:T(8,128)S(1)}, f32[18,2,64,128]{3,2,1,0:T(8,128)S(1)}, s32[]{:T(128)}, ...), condition=%wide.region_1.2_spmd, body=%wide.region_0.1_spmd.sunk | while | flops 404095008 | bytes 9634135 | solution.py:37
  4.6 0.4 slice_negate_fusion.4
  4.9 1.2 copy.22
  6.2 3.1 %fusion.26 = f32[32,64,128]{2,1,0:T(8,128)} fusion(f32[32,64,128]{2,1,0:T(8,128)S(1)} %copy.22, f32[32,64,64]{2,1,0:T(8,128)S(1)} %get-tuple-element.256, f32[32,64,64]{2,1,0:T(8,128)S(1)} %get-tuple-element.257, f32[32,64,128]{2,1,0:T(8,128)S(1)} %broadcast_select_fusion.3), kind=kOutput, calls=%fused_computation.7.clone.1 | convolution fusion | flops 403701760 | bytes 4194304 | tf_op jit(solution)/shard_map/while/body/eval_jaxpr/bij,bjk->bik/dot_general | solution.py:14
  9.5 0.4 slice_negate_fusion.4
  9.8 1.2 copy.22
  11.1 3.1 %fusion.26 = f32[32,64,128]{2,1,0:T(8,128)} fusion(f32[32,64,128]{2,1,0:T(8,128)S(1)} %copy.22, f32[32,64,64]{2,1,0:T(8,128)S(1)} %get-tuple-element.256, f32[32,64,64]{2,1,0:T(8,128)S(1)} %get-tuple-element.257, f32[32,64,128]{2,1,0:T(8,128)S(1)} %broadcast_select_fusion.3), kind=kOutput, calls=%fused_computation.7.clone.1 | convolution fusion | flops 403701760 | bytes 4194304 | tf_op jit(solution)/shard_map/while/body/eval_jaxpr/bij,bjk->bik/dot_general | solution.py:14
  14.3 0.4 slice_negate_fusion.4
  14.7 1.2 copy.22
  16.0 3.1 %fusion.26 = f32[32,64,128]{2,1,0:T(8,128)} fusion(f32[32,64,128]{2,1,0:T(8,128)S(1)} %copy.22, f32[32,64,64]{2,1,0:T(8,128)S(1)} %get-tuple-element.256, f32[32,64,64]{2,1,0:T(8,128)S(1)} %get-tuple-element.257, f32[32,64,128]{2,1,0:T(8,128)S(1)} %broadcast_select_fusion.3), kind=kOutput, calls=%fused_computation.7.clone.1 | convolution fusion | flops 403701760 | bytes 4194304 | tf_op jit(solution)/shard_map/while/body/eval_jaxpr/bij,bjk->bik/dot_general | solution.py:14
  19.2 0.4 slice_negate_fusion.4
  19.6 1.2 copy.22
  20.9 3.1 %fusion.26 = f32[32,64,128]{2,1,0:T(8,128)} fusion(f32[32,64,128]{2,1,0:T(8,128)S(1)} %copy.22, f32[32,64,64]{2,1,0:T(8,128)S(1)} %get-tuple-element.256, f32[32,64,64]{2,1,0:T(8,128)S(1)} %get-tuple-element.257, f32[32,64,128]{2,1,0:T(8,128)S(1)} %broadcast_select_fusion.3), kind=kOutput, calls=%fused_computation.7.clone.1 | convolution fusion | flops 403701760 | bytes 4194304 | tf_op jit(solution)/shard_map/while/body/eval_jaxpr/bij,bjk->bik/dot_general | solution.py:14
  24.1 0.4 slice_negate_fusion.4
  24.5 1.2 copy.22
  25.8 3.1 %fusion.26 = f32[32,64,128]{2,1,0:T(8,128)} fusion(f32[32,64,128]{2,1,0:T(8,128)S(1)} %copy.22, f32[32,64,64]{2,1,0:T(8,128)S(1)} %get-tuple-element.256, f32[32,64,64]{2,1,0:T(8,128)S(1)} %get-tuple-element.257, f32[32,64,128]{2,1,0:T(8,128)S(1)} %broadcast_select_fusion.3), kind=kOutput, calls=%fused_computation.7.clone.1 | convolution fusion | flops 403701760 | bytes 4194304 | tf_op jit(solution)/shard_map/while/body/eval_jaxpr/bij,bjk->bik/dot_general | solution.py:14
  29.0 0.4 slice_negate_fusion.4
  29.4 1.2 copy.22
  30.7 3.1 %fusion.26 = f32[32,64,128]{2,1,0:T(8,128)} fusion(f32[32,64,128]{2,1,0:T(8,128)S(1)} %copy.22, f32[32,64,64]{2,1,0:T(8,128)S(1)} %get-tuple-element.256, f32[32,64,64]{2,1,0:T(8,128)S(1)} %get-tuple-element.257, f32[32,64,128]{2,1,0:T(8,128)S(1)} %broadcast_select_fusion.3), kind=kOutput, calls=%fused_computation.7.clone.1 | convolution fusion | flops 403701760 | bytes 4194304 | tf_op jit(solution)/shard_map/while/body/eval_jaxpr/bij,bjk->bik/dot_general | solution.py:14
  33.9 0.4 slice_negate_fusion.4
  34.3 1.2 copy.22
  35.5 3.1 %fusion.26 = f32[32,64,128]{2,1,0:T(8,128)} fusion(f32[32,64,128]{2,1,0:T(8,128)S(1)} %copy.22, f32[32,64,64]{2,1,0:T(8,128)S(1)} %get-tuple-element.256, f32[32,64,64]{2,1,0:T(8,128)S(1)} %get-tuple-element.257, f32[32,64,128]{2,1,0:T(8,128)S(1)} %broadcast_select_fusion.3), kind=kOutput, calls=%fused_computation.7.clone.1 | convolution fusion | flops 403701760 | bytes 4194304 | tf_op jit(solution)/shard_map/while/body/eval_jaxpr/bij,bjk->bik/dot_general | solution.py:14
  38.8 0.4 slice_negate_fusion.4
  39.2 1.2 copy.22
  40.4 3.1 %fusion.26 = f32[32,64,128]{2,1,0:T(8,128)} fusion(f32[32,64,128]{2,1,0:T(8,128)S(1)} %copy.22, f32[32,64,64]{2,1,0:T(8,128)S(1)} %get-tuple-element.256, f32[32,64,64]{2,1,0:T(8,128)S(1)} %get-tuple-element.257, f32[32,64,128]{2,1,0:T(8,128)S(1)} %broadcast_select_fusion.3), kind=kOutput, calls=%fused_computation.7.clone.1 | convolution fusion | flops 403701760 | bytes 4194304 | tf_op jit(solution)/shard_map/while/body/eval_jaxpr/bij,bjk->bik/dot_general | solution.py:14
  43.7 0.4 slice_negate_fusion.4
  44.1 1.2 copy.22
  45.3 3.1 %fusion.26 = f32[32,64,128]{2,1,0:T(8,128)} fusion(f32[32,64,128]{2,1,0:T(8,128)S(1)} %copy.22, f32[32,64,64]{2,1,0:T(8,128)S(1)} %get-tuple-element.256, f32[32,64,64]{2,1,0:T(8,128)S(1)} %get-tuple-element.257, f32[32,64,128]{2,1,0:T(8,128)S(1)} %broadcast_select_fusion.3), kind=kOutput, calls=%fused_computation.7.clone.1 | convolution fusion | flops 403701760 | bytes 4194304 | tf_op jit(solution)/shard_map/while/body/eval_jaxpr/bij,bjk->bik/dot_general | solution.py:14
  48.6 0.4 slice_negate_fusion.4
  49.0 1.2 copy.22
  50.2 3.1 %fusion.26 = f32[32,64,128]{2,1,0:T(8,128)} fusion(f32[32,64,128]{2,1,0:T(8,128)S(1)} %copy.22, f32[32,64,64]{2,1,0:T(8,128)S(1)} %get-tuple-element.256, f32[32,64,64]{2,1,0:T(8,128)S(1)} %get-tuple-element.257, f32[32,64,128]{2,1,0:T(8,128)S(1)} %broadcast_select_fusion.3), kind=kOutput, calls=%fused_computation.7.clone.1 | convolution fusion | flops 403701760 | bytes 4194304 | tf_op jit(solution)/shard_map/while/body/eval_jaxpr/bij,bjk->bik/dot_general | solution.py:14
  53.5 0.4 slice_negate_fusion.4
  53.9 1.2 copy.22
  55.1 3.1 %fusion.26 = f32[32,64,128]{2,1,0:T(8,128)} fusion(f32[32,64,128]{2,1,0:T(8,128)S(1)} %copy.22, f32[32,64,64]{2,1,0:T(8,128)S(1)} %get-tuple-element.256, f32[32,64,64]{2,1,0:T(8,128)S(1)} %get-tuple-element.257, f32[32,64,128]{2,1,0:T(8,128)S(1)} %broadcast_select_fusion.3), kind=kOutput, calls=%fused_computation.7.clone.1 | convolution fusion | flops 403701760 | bytes 4194304 | tf_op jit(solution)/shard_map/while/body/eval_jaxpr/bij,bjk->bik/dot_general | solution.py:14
  58.4 0.4 slice_negate_fusion.4
  58.8 1.2 copy.22
  60.0 3.1 %fusion.26 = f32[32,64,128]{2,1,0:T(8,128)} fusion(f32[32,64,128]{2,1,0:T(8,128)S(1)} %copy.22, f32[32,64,64]{2,1,0:T(8,128)S(1)} %get-tuple-element.256, f32[32,64,64]{2,1,0:T(8,128)S(1)} %get-tuple-element.257, f32[32,64,128]{2,1,0:T(8,128)S(1)} %broadcast_select_fusion.3), kind=kOutput, calls=%fused_computation.7.clone.1 | convolution fusion | flops 403701760 | bytes 4194304 | tf_op jit(solution)/shard_map/while/body/eval_jaxpr/bij,bjk->bik/dot_general | solution.py:14
  63.3 0.4 slice_negate_fusion.4
  63.7 1.2 copy.22
  64.9 3.1 %fusion.26 = f32[32,64,128]{2,1,0:T(8,128)} fusion(f32[32,64,128]{2,1,0:T(8,128)S(1)} %copy.22, f32[32,64,64]{2,1,0:T(8,128)S(1)} %get-tuple-element.256, f32[32,64,64]{2,1,0:T(8,128)S(1)} %get-tuple-element.257, f32[32,64,128]{2,1,0:T(8,128)S(1)} %broadcast_select_fusion.3), kind=kOutput, calls=%fused_computation.7.clone.1 | convolution fusion | flops 403701760 | bytes 4194304 | tf_op jit(solution)/shard_map/while/body/eval_jaxpr/bij,bjk->bik/dot_general | solution.py:14
  68.2 0.4 slice_negate_fusion.4
  68.6 1.2 copy.22
  69.8 3.1 %fusion.26 = f32[32,64,128]{2,1,0:T(8,128)} fusion(f32[32,64,128]{2,1,0:T(8,128)S(1)} %copy.22, f32[32,64,64]{2,1,0:T(8,128)S(1)} %get-tuple-element.256, f32[32,64,64]{2,1,0:T(8,128)S(1)} %get-tuple-element.257, f32[32,64,128]{2,1,0:T(8,128)S(1)} %broadcast_select_fusion.3), kind=kOutput, calls=%fused_computation.7.clone.1 | convolution fusion | flops 403701760 | bytes 4194304 | tf_op jit(solution)/shard_map/while/body/eval_jaxpr/bij,bjk->bik/dot_general | solution.py:14
  73.1 0.4 slice_negate_fusion.4
  73.5 1.2 copy.22
  74.7 3.1 %fusion.26 = f32[32,64,128]{2,1,0:T(8,128)} fusion(f32[32,64,128]{2,1,0:T(8,128)S(1)} %copy.22, f32[32,64,64]{2,1,0:T(8,128)S(1)} %get-tuple-element.256, f32[32,64,64]{2,1,0:T(8,128)S(1)} %get-tuple-element.257, f32[32,64,128]{2,1,0:T(8,128)S(1)} %broadcast_select_fusion.3), kind=kOutput, calls=%fused_computation.7.clone.1 | convolution fusion | flops 403701760 | bytes 4194304 | tf_op jit(solution)/shard_map/while/body/eval_jaxpr/bij,bjk->bik/dot_general | solution.py:14
  78.4 1.2 copy.22
  79.6 3.1 %fusion.26 = f32[32,64,128]{2,1,0:T(8,128)} fusion(f32[32,64,128]{2,1,0:T(8,128)S(1)} %copy.22, f32[32,64,64]{2,1,0:T(8,128)S(1)} %get-tuple-element.256, f32[32,64,64]{2,1,0:T(8,128)S(1)} %get-tuple-element.257, f32[32,64,128]{2,1,0:T(8,128)S(1)} %broadcast_select_fusion.3), kind=kOutput, calls=%fused_computation.7.clone.1 | convolution fusion | flops 403701760 | bytes 4194304 | tf_op jit(solution)/shard_map/while/body/eval_jaxpr/bij,bjk->bik/dot_general | solution.py:14
  82.9 0.4 slice_negate_fusion.4
  83.3 1.2 copy.22
  84.5 3.1 %fusion.26 = f32[32,64,128]{2,1,0:T(8,128)} fusion(f32[32,64,128]{2,1,0:T(8,128)S(1)} %copy.22, f32[32,64,64]{2,1,0:T(8,128)S(1)} %get-tuple-element.256, f32[32,64,64]{2,1,0:T(8,128)S(1)} %get-tuple-element.257, f32[32,64,128]{2,1,0:T(8,128)S(1)} %broadcast_select_fusion.3), kind=kOutput, calls=%fused_computation.7.clone.1 | convolution fusion | flops 403701760 | bytes 4194304 | tf_op jit(solution)/shard_map/while/body/eval_jaxpr/bij,bjk->bik/dot_general | solution.py:14
  87.6 6.5 %all-to-all-start = ((f32[4,8,64,128]{3,2,1,0:T(8,128)}), f32[4,8,64,128]{3,2,1,0:T(8,128)S(1)}, u32[]{:S(2)}, u32[]{:S(2)}) async-start(f32[4,8,64,128]{3,2,1,0:T(8,128)} %bitcast.13), calls=%async_computation | async-start | bytes 2097152 | tf_op jit(solution)/shard_map/all_to_all | solution.py:58
  94.2 25.6 %all-to-all-done = f32[4,8,64,128]{3,2,1,0:T(8,128)S(1)} async-done(((f32[4,8,64,128]{3,2,1,0:T(8,128)}), f32[4,8,64,128]{3,2,1,0:T(8,128)S(1)}, u32[]{:S(2)}, u32[]{:S(2)}) %all-to-all-start) | async-done | bytes 1048608 | tf_op jit(solution)/shard_map/all_to_all | solution.py:58
  119.8 3.4 %while.29 = (s32[]{:T(128)}, f32[8,64,128]{2,1,0:T(8,128)S(1)}, f32[4,8,64,128]{3,2,1,0:T(8,128)S(1)}, s32[]{:T(128)}) while((s32[]{:T(128)}, f32[8,64,128]{2,1,0:T(8,128)S(1)}, f32[4,8,64,128]{3,2,1,0:T(8,128)S(1)}, s32[]{:T(128)}) %tuple.74), condition=%wide.region_3.4_spmd, body=%wide.region_2.3_spmd.sunk | while | flops 100958208 | bytes 2621497 | solution.py:61
  120.1 0.6 convolution_bitcast_fusion.2
  120.9 0.6 convolution_bitcast_fusion.2
  121.8 0.6 convolution_bitcast_fusion.2
  122.6 0.6 convolution_bitcast_fusion.2
  123.7 20.2 %psum.7 = f32[2,32]{1,0:T(2,128)} all-reduce(f32[2,32]{1,0:T(2,128)S(1)} %dynamic_update_slice.3), channel_id=1, replica_groups=mesh['grp'=2,'col'=4,'slc'=2,'bat'=2] {'col','slc'}, use_global_device_ids=true, to_apply=%region_6.7 | all-reduce | flops 64 | bytes 512 | tf_op jit(solution)/shard_map/psum | solution.py:73
  (81 shorter events, 4.3 us)
Async XLA Ops:
  0.0 2.5 %copy-start.2 = (s32[32,72]{1,0:T(8,128)S(1)}, s32[32,72]{1,0:T(8,128)}, u32[]{:S(2)}) copy-start(s32[32,72]{1,0:T(8,128)} %param.13) | copy-start | bytes 27652
  87.6 6.5 %copy-start = (f32[1,64,128]{2,1,0:T(8,128)S(1)}, f32[1,64,128]{2,1,0:T(8,128)}, u32[]{:S(2)}) copy-start(f32[1,64,128]{2,1,0:T(8,128)} %param.11) | copy-start | bytes 98308
  87.6 32.2 %copy-start.1 = (f32[1,64,128]{2,1,0:T(8,128)S(1)}, f32[1,64,128]{2,1,0:T(8,128)}, u32[]{:S(2)}) copy-start(f32[1,64,128]{2,1,0:T(8,128)} %param.10) | copy-start | bytes 98308
  87.6 32.2 %all-to-all-start = ((f32[4,8,64,128]{3,2,1,0:T(8,128)}), f32[4,8,64,128]{3,2,1,0:T(8,128)S(1)}, u32[]{:S(2)}, u32[]{:S(2)}) async-start(f32[4,8,64,128]{3,2,1,0:T(8,128)} %bitcast.13), calls=%async_computation | async-start | bytes 2097152 | tf_op jit(solution)/shard_map/all_to_all | solution.py:58
where the time goes:
time: 145 us; the launch traced here: 144 us
  matrix products  55.4 us (38%)
  waiting for transfers between devices  25.6 us (18%)
  local copies, waits for them, and re-layouts  22.1 us (15%)
  blocking collectives  20.2 us (14%)
  other arithmetic  13.5 us (9%)
  starting transfers between devices  6.48 us (4%)
    dot_general x21, matrix products, complex_product(): jnp.einsum('bij,bjk->bik', first_factor, stacked, precision=lax.Precision...  55.4 us
    all_to_all x1, waiting for transfers between devices, on_device(): lax.all_to_all(grouped, 'col', split_axis=0, concat_axis=0, tiled=True)  25.6 us
    while x21, local copies, waits for them, and re-layouts  21 us
    psum x1, blocking collectives, on_device(): return lax.psum(placed, ('col', 'slc'))  20.2 us
    neg x21, other arithmetic, rotate(): return jnp.concatenate([-block[..., middle:], block[..., :middle]], axis=-1)  7.05 us
    all_to_all x1, starting transfers between devices, on_device(): lax.all_to_all(grouped, 'col', split_axis=0, concat_axis=0, tiled=True)  6.48 us
    select_n x18, other arithmetic, select_site(): return jnp.where(chosen_bits[:, None, None] == 1, matrices[1], matrices[0])  3.41 us
  transfers between devices with their start and end apart: 1, of which 1 were waited for; matrix products, arithmetic and copies ran while one was open for 0% of the time, Pallas kernels for 0%

commit v1 on v0

--- a/solution.py
+++ b/solution.py
@@ -70,7 +70,7 @@
     placed = lax.dynamic_update_slice(
         jnp.zeros((2, padded_rows), jnp.float32), closed, (jnp.int32(0), col_index * share)
     )
-    return lax.psum(placed, ("col", "slc"))
+    return lax.psum(lax.psum(placed, axis_name="slc"), axis_name="col")
 
 
 def solution(mesh):

time: 145 us -> 140 us (0.966)
  blocking collectives: 20.2 us -> 15.4 us
    psum x1 -> x2, blocking collectives: 20.2 us -> 15.4 us  [on_device(): return lax.psum(lax.psum(placed, axis_name='slc'), axis_name='col')]
where the time goes in v1:
time: 140 us; the launch traced here: 139 us
  matrix products  55.6 us (40%)
  waiting for transfers between devices  25.6 us (18%)
  local copies, waits for them, and re-layouts  22.1 us (16%)
  blocking collectives  15.4 us (11%)
  other arithmetic  13.5 us (10%)
  starting transfers between devices  6.48 us (5%)
    dot_general x21, matrix products, complex_product(): jnp.einsum('bij,bjk->bik', first_factor, stacked, precision=lax.Precision...  55.6 us
    all_to_all x1, waiting for transfers between devices, on_device(): lax.all_to_all(grouped, 'col', split_axis=0, concat_axis=0, tiled=True)  25.6 us
    while x21, local copies, waits for them, and re-layouts  21 us
    psum x2, blocking collectives, on_device(): return lax.psum(lax.psum(placed, axis_name='slc'), axis_name='col')  15.4 us
    neg x21, other arithmetic, rotate(): return jnp.concatenate([-block[..., middle:], block[..., :middle]], axis=-1)  7.05 us
    all_to_all x1, starting transfers between devices, on_device(): lax.all_to_all(grouped, 'col', split_axis=0, concat_axis=0, tiled=True)  6.48 us
    select_n x18, other arithmetic, select_site(): return jnp.where(chosen_bits[:, None, None] == 1, matrices[1], matrices[0])  3.42 us
  transfers between devices with their start and end apart: 1, of which 1 were waited for; matrix products, arithmetic and copies ran while one was open for 0% of the time, Pallas kernels for 0%

profile of v1, /device:TPU:0, one launch (start us, length us, event | category | flops | bytes accessed | tf_op | source)
XLA Modules:
  0.0 139.3 jit_solution(13303900282027215822)
XLA Ops:
  0.0 0.7 compare_select_fusion
  0.7 0.7 compare_and_fusion
  1.3 1.2 bitcast_convert_fusion
  2.6 0.6 gather_fusion
  3.3 1.1 broadcast_select_fusion.1
  4.4 83.4 %while.28 = (s32[]{:T(128)}, f32[32,64,128]{2,1,0:T(8,128)}, s32[32,18]{0,1:T(8,128)S(1)}, f32[18,2,64,128]{3,2,1,0:T(8,128)S(1)}, s32[]{:T(128)}, /*index=5*/s32[]{:T(128)}, s32[]{:T(128)}, s32[]{}) while((s32[]{:T(128)}, f32[32,64,128]{2,1,0:T(8,128)}, s32[32,18]{0,1:T(8,128)S(1)}, f32[18,2,64,128]{3,2,1,0:T(8,128)S(1)}, s32[]{:T(128)}, ...), condition=%wide.region_1.2_spmd, body=%wide.region_0.1_spmd.sunk | while | flops 404095008 | bytes 9634135 | solution.py:37
  4.6 0.4 slice_negate_fusion.4
  5.0 1.2 copy.22
  6.2 3.1 %fusion.26 = f32[32,64,128]{2,1,0:T(8,128)} fusion(f32[32,64,128]{2,1,0:T(8,128)S(1)} %copy.22, f32[32,64,64]{2,1,0:T(8,128)S(1)} %get-tuple-element.256, f32[32,64,64]{2,1,0:T(8,128)S(1)} %get-tuple-element.257, f32[32,64,128]{2,1,0:T(8,128)S(1)} %broadcast_select_fusion.3), kind=kOutput, calls=%fused_computation.7.clone.1 | convolution fusion | flops 403701760 | bytes 4194304 | tf_op jit(solution)/shard_map/while/body/eval_jaxpr/bij,bjk->bik/dot_general | solution.py:14
  9.5 0.4 slice_negate_fusion.4
  9.9 1.2 copy.22
  11.1 3.1 %fusion.26 = f32[32,64,128]{2,1,0:T(8,128)} fusion(f32[32,64,128]{2,1,0:T(8,128)S(1)} %copy.22, f32[32,64,64]{2,1,0:T(8,128)S(1)} %get-tuple-element.256, f32[32,64,64]{2,1,0:T(8,128)S(1)} %get-tuple-element.257, f32[32,64,128]{2,1,0:T(8,128)S(1)} %broadcast_select_fusion.3), kind=kOutput, calls=%fused_computation.7.clone.1 | convolution fusion | flops 403701760 | bytes 4194304 | tf_op jit(solution)/shard_map/while/body/eval_jaxpr/bij,bjk->bik/dot_general | solution.py:14
  14.4 0.4 slice_negate_fusion.4
  14.8 1.2 copy.22
  16.0 3.1 %fusion.26 = f32[32,64,128]{2,1,0:T(8,128)} fusion(f32[32,64,128]{2,1,0:T(8,128)S(1)} %copy.22, f32[32,64,64]{2,1,0:T(8,128)S(1)} %get-tuple-element.256, f32[32,64,64]{2,1,0:T(8,128)S(1)} %get-tuple-element.257, f32[32,64,128]{2,1,0:T(8,128)S(1)} %broadcast_select_fusion.3), kind=kOutput, calls=%fused_computation.7.clone.1 | convolution fusion | flops 403701760 | bytes 4194304 | tf_op jit(solution)/shard_map/while/body/eval_jaxpr/bij,bjk->bik/dot_general | solution.py:14
  19.3 0.4 slice_negate_fusion.4
  19.7 1.2 copy.22
  20.9 3.1 %fusion.26 = f32[32,64,128]{2,1,0:T(8,128)} fusion(f32[32,64,128]{2,1,0:T(8,128)S(1)} %copy.22, f32[32,64,64]{2,1,0:T(8,128)S(1)} %get-tuple-element.256, f32[32,64,64]{2,1,0:T(8,128)S(1)} %get-tuple-element.257, f32[32,64,128]{2,1,0:T(8,128)S(1)} %broadcast_select_fusion.3), kind=kOutput, calls=%fused_computation.7.clone.1 | convolution fusion | flops 403701760 | bytes 4194304 | tf_op jit(solution)/shard_map/while/body/eval_jaxpr/bij,bjk->bik/dot_general | solution.py:14
  24.2 0.4 slice_negate_fusion.4
  24.6 1.2 copy.22
  25.8 3.1 %fusion.26 = f32[32,64,128]{2,1,0:T(8,128)} fusion(f32[32,64,128]{2,1,0:T(8,128)S(1)} %copy.22, f32[32,64,64]{2,1,0:T(8,128)S(1)} %get-tuple-element.256, f32[32,64,64]{2,1,0:T(8,128)S(1)} %get-tuple-element.257, f32[32,64,128]{2,1,0:T(8,128)S(1)} %broadcast_select_fusion.3), kind=kOutput, calls=%fused_computation.7.clone.1 | convolution fusion | flops 403701760 | bytes 4194304 | tf_op jit(solution)/shard_map/while/body/eval_jaxpr/bij,bjk->bik/dot_general | solution.py:14
  29.1 0.4 slice_negate_fusion.4
  29.5 1.2 copy.22
  30.7 3.1 %fusion.26 = f32[32,64,128]{2,1,0:T(8,128)} fusion(f32[32,64,128]{2,1,0:T(8,128)S(1)} %copy.22, f32[32,64,64]{2,1,0:T(8,128)S(1)} %get-tuple-element.256, f32[32,64,64]{2,1,0:T(8,128)S(1)} %get-tuple-element.257, f32[32,64,128]{2,1,0:T(8,128)S(1)} %broadcast_select_fusion.3), kind=kOutput, calls=%fused_computation.7.clone.1 | convolution fusion | flops 403701760 | bytes 4194304 | tf_op jit(solution)/shard_map/while/body/eval_jaxpr/bij,bjk->bik/dot_general | solution.py:14
  34.0 0.4 slice_negate_fusion.4
  34.4 1.2 copy.22
  35.6 3.1 %fusion.26 = f32[32,64,128]{2,1,0:T(8,128)} fusion(f32[32,64,128]{2,1,0:T(8,128)S(1)} %copy.22, f32[32,64,64]{2,1,0:T(8,128)S(1)} %get-tuple-element.256, f32[32,64,64]{2,1,0:T(8,128)S(1)} %get-tuple-element.257, f32[32,64,128]{2,1,0:T(8,128)S(1)} %broadcast_select_fusion.3), kind=kOutput, calls=%fused_computation.7.clone.1 | convolution fusion | flops 403701760 | bytes 4194304 | tf_op jit(solution)/shard_map/while/body/eval_jaxpr/bij,bjk->bik/dot_general | solution.py:14
  38.9 0.4 slice_negate_fusion.4
  39.3 1.2 copy.22
  40.5 3.1 %fusion.26 = f32[32,64,128]{2,1,0:T(8,128)} fusion(f32[32,64,128]{2,1,0:T(8,128)S(1)} %copy.22, f32[32,64,64]{2,1,0:T(8,128)S(1)} %get-tuple-element.256, f32[32,64,64]{2,1,0:T(8,128)S(1)} %get-tuple-element.257, f32[32,64,128]{2,1,0:T(8,128)S(1)} %broadcast_select_fusion.3), kind=kOutput, calls=%fused_computation.7.clone.1 | convolution fusion | flops 403701760 | bytes 4194304 | tf_op jit(solution)/shard_map/while/body/eval_jaxpr/bij,bjk->bik/dot_general | solution.py:14
  43.8 0.4 slice_negate_fusion.4
  44.2 1.2 copy.22
  45.4 3.1 %fusion.26 = f32[32,64,128]{2,1,0:T(8,128)} fusion(f32[32,64,128]{2,1,0:T(8,128)S(1)} %copy.22, f32[32,64,64]{2,1,0:T(8,128)S(1)} %get-tuple-element.256, f32[32,64,64]{2,1,0:T(8,128)S(1)} %get-tuple-element.257, f32[32,64,128]{2,1,0:T(8,128)S(1)} %broadcast_select_fusion.3), kind=kOutput, calls=%fused_computation.7.clone.1 | convolution fusion | flops 403701760 | bytes 4194304 | tf_op jit(solution)/shard_map/while/body/eval_jaxpr/bij,bjk->bik/dot_general | solution.py:14
  48.7 0.4 slice_negate_fusion.4
  49.1 1.2 copy.22
  50.4 3.1 %fusion.26 = f32[32,64,128]{2,1,0:T(8,128)} fusion(f32[32,64,128]{2,1,0:T(8,128)S(1)} %copy.22, f32[32,64,64]{2,1,0:T(8,128)S(1)} %get-tuple-element.256, f32[32,64,64]{2,1,0:T(8,128)S(1)} %get-tuple-element.257, f32[32,64,128]{2,1,0:T(8,128)S(1)} %broadcast_select_fusion.3), kind=kOutput, calls=%fused_computation.7.clone.1 | convolution fusion | flops 403701760 | bytes 4194304 | tf_op jit(solution)/shard_map/while/body/eval_jaxpr/bij,bjk->bik/dot_general | solution.py:14
  53.6 0.4 slice_negate_fusion.4
  54.0 1.2 copy.22
  55.3 3.1 %fusion.26 = f32[32,64,128]{2,1,0:T(8,128)} fusion(f32[32,64,128]{2,1,0:T(8,128)S(1)} %copy.22, f32[32,64,64]{2,1,0:T(8,128)S(1)} %get-tuple-element.256, f32[32,64,64]{2,1,0:T(8,128)S(1)} %get-tuple-element.257, f32[32,64,128]{2,1,0:T(8,128)S(1)} %broadcast_select_fusion.3), kind=kOutput, calls=%fused_computation.7.clone.1 | convolution fusion | flops 403701760 | bytes 4194304 | tf_op jit(solution)/shard_map/while/body/eval_jaxpr/bij,bjk->bik/dot_general | solution.py:14
  58.9 1.2 copy.22
  60.2 3.1 %fusion.26 = f32[32,64,128]{2,1,0:T(8,128)} fusion(f32[32,64,128]{2,1,0:T(8,128)S(1)} %copy.22, f32[32,64,64]{2,1,0:T(8,128)S(1)} %get-tuple-element.256, f32[32,64,64]{2,1,0:T(8,128)S(1)} %get-tuple-element.257, f32[32,64,128]{2,1,0:T(8,128)S(1)} %broadcast_select_fusion.3), kind=kOutput, calls=%fused_computation.7.clone.1 | convolution fusion | flops 403701760 | bytes 4194304 | tf_op jit(solution)/shard_map/while/body/eval_jaxpr/bij,bjk->bik/dot_general | solution.py:14
  63.5 0.4 slice_negate_fusion.4
  63.8 1.2 copy.22
  65.1 3.1 %fusion.26 = f32[32,64,128]{2,1,0:T(8,128)} fusion(f32[32,64,128]{2,1,0:T(8,128)S(1)} %copy.22, f32[32,64,64]{2,1,0:T(8,128)S(1)} %get-tuple-element.256, f32[32,64,64]{2,1,0:T(8,128)S(1)} %get-tuple-element.257, f32[32,64,128]{2,1,0:T(8,128)S(1)} %broadcast_select_fusion.3), kind=kOutput, calls=%fused_computation.7.clone.1 | convolution fusion | flops 403701760 | bytes 4194304 | tf_op jit(solution)/shard_map/while/body/eval_jaxpr/bij,bjk->bik/dot_general | solution.py:14
  68.4 0.4 slice_negate_fusion.4
  68.7 1.2 copy.22
  70.0 3.1 %fusion.26 = f32[32,64,128]{2,1,0:T(8,128)} fusion(f32[32,64,128]{2,1,0:T(8,128)S(1)} %copy.22, f32[32,64,64]{2,1,0:T(8,128)S(1)} %get-tuple-element.256, f32[32,64,64]{2,1,0:T(8,128)S(1)} %get-tuple-element.257, f32[32,64,128]{2,1,0:T(8,128)S(1)} %broadcast_select_fusion.3), kind=kOutput, calls=%fused_computation.7.clone.1 | convolution fusion | flops 403701760 | bytes 4194304 | tf_op jit(solution)/shard_map/while/body/eval_jaxpr/bij,bjk->bik/dot_general | solution.py:14
  73.7 1.2 copy.22
  74.9 3.1 %fusion.26 = f32[32,64,128]{2,1,0:T(8,128)} fusion(f32[32,64,128]{2,1,0:T(8,128)S(1)} %copy.22, f32[32,64,64]{2,1,0:T(8,128)S(1)} %get-tuple-element.256, f32[32,64,64]{2,1,0:T(8,128)S(1)} %get-tuple-element.257, f32[32,64,128]{2,1,0:T(8,128)S(1)} %broadcast_select_fusion.3), kind=kOutput, calls=%fused_computation.7.clone.1 | convolution fusion | flops 403701760 | bytes 4194304 | tf_op jit(solution)/shard_map/while/body/eval_jaxpr/bij,bjk->bik/dot_general | solution.py:14
  78.2 0.4 slice_negate_fusion.4
  78.6 1.2 copy.22
  79.8 3.1 %fusion.26 = f32[32,64,128]{2,1,0:T(8,128)} fusion(f32[32,64,128]{2,1,0:T(8,128)S(1)} %copy.22, f32[32,64,64]{2,1,0:T(8,128)S(1)} %get-tuple-element.256, f32[32,64,64]{2,1,0:T(8,128)S(1)} %get-tuple-element.257, f32[32,64,128]{2,1,0:T(8,128)S(1)} %broadcast_select_fusion.3), kind=kOutput, calls=%fused_computation.7.clone.1 | convolution fusion | flops 403701760 | bytes 4194304 | tf_op jit(solution)/shard_map/while/body/eval_jaxpr/bij,bjk->bik/dot_general | solution.py:14
  83.1 0.4 slice_negate_fusion.4
  83.5 1.2 copy.22
  84.7 3.1 %fusion.26 = f32[32,64,128]{2,1,0:T(8,128)} fusion(f32[32,64,128]{2,1,0:T(8,128)S(1)} %copy.22, f32[32,64,64]{2,1,0:T(8,128)S(1)} %get-tuple-element.256, f32[32,64,64]{2,1,0:T(8,128)S(1)} %get-tuple-element.257, f32[32,64,128]{2,1,0:T(8,128)S(1)} %broadcast_select_fusion.3), kind=kOutput, calls=%fused_computation.7.clone.1 | convolution fusion | flops 403701760 | bytes 4194304 | tf_op jit(solution)/shard_map/while/body/eval_jaxpr/bij,bjk->bik/dot_general | solution.py:14
  87.8 6.5 %all-to-all-start = ((f32[4,8,64,128]{3,2,1,0:T(8,128)}), f32[4,8,64,128]{3,2,1,0:T(8,128)S(1)}, u32[]{:S(2)}, u32[]{:S(2)}) async-start(f32[4,8,64,128]{3,2,1,0:T(8,128)} %bitcast.13), calls=%async_computation | async-start | bytes 2097152 | tf_op jit(solution)/shard_map/all_to_all | solution.py:58
  94.4 25.6 %all-to-all-done = f32[4,8,64,128]{3,2,1,0:T(8,128)S(1)} async-done(((f32[4,8,64,128]{3,2,1,0:T(8,128)}), f32[4,8,64,128]{3,2,1,0:T(8,128)S(1)}, u32[]{:S(2)}, u32[]{:S(2)}) %all-to-all-start) | async-done | bytes 1048608 | tf_op jit(solution)/shard_map/all_to_all | solution.py:58
  120.1 3.4 %while.29 = (s32[]{:T(128)}, f32[8,64,128]{2,1,0:T(8,128)S(1)}, f32[4,8,64,128]{3,2,1,0:T(8,128)S(1)}, s32[]{:T(128)}) while((s32[]{:T(128)}, f32[8,64,128]{2,1,0:T(8,128)S(1)}, f32[4,8,64,128]{3,2,1,0:T(8,128)S(1)}, s32[]{:T(128)}) %tuple.74), condition=%wide.region_3.4_spmd, body=%wide.region_2.3_spmd.sunk | while | flops 100958208 | bytes 2621497 | solution.py:61
  120.3 0.6 convolution_bitcast_fusion.2
  121.1 0.6 convolution_bitcast_fusion.2
  122.0 0.6 convolution_bitcast_fusion.2
  122.8 0.6 convolution_bitcast_fusion.2
  123.9 4.9 %psum.14 = f32[2,32]{1,0:T(2,128)S(1)} all-reduce(f32[2,32]{1,0:T(2,128)S(1)} %dynamic_update_slice.3), channel_id=1, replica_groups=mesh['grp'=2,'col'=4,'slc'=2,'bat'=2] {'slc'}, use_global_device_ids=true, to_apply=%region_6.7 | all-reduce | flops 64 | bytes 512 | tf_op jit(solution)/shard_map/psum | solution.py:73
  128.8 10.5 %psum.15 = f32[2,32]{1,0:T(2,128)} all-reduce(f32[2,32]{1,0:T(2,128)S(1)} %psum.14), channel_id=1, replica_groups=mesh['grp'=2,'col'=4,'slc'=2,'bat'=2] {'col'}, use_global_device_ids=true, to_apply=%region_7.8 | all-reduce | flops 64 | bytes 512 | tf_op jit(solution)/shard_map/psum | solution.py:73
  (82 shorter events, 4.7 us)
Async XLA Ops:
  0.0 2.5 %copy-start.2 = (s32[32,72]{1,0:T(8,128)S(1)}, s32[32,72]{1,0:T(8,128)}, u32[]{:S(2)}) copy-start(s32[32,72]{1,0:T(8,128)} %param.13) | copy-start | bytes 27652
  87.8 6.5 %copy-start = (f32[1,64,128]{2,1,0:T(8,128)S(1)}, f32[1,64,128]{2,1,0:T(8,128)}, u32[]{:S(2)}) copy-start(f32[1,64,128]{2,1,0:T(8,128)} %param.11) | copy-start | bytes 98308
  87.8 32.2 %copy-start.1 = (f32[1,64,128]{2,1,0:T(8,128)S(1)}, f32[1,64,128]{2,1,0:T(8,128)}, u32[]{:S(2)}) copy-start(f32[1,64,128]{2,1,0:T(8,128)} %param.10) | copy-start | bytes 98308
  87.8 32.2 %all-to-all-start = ((f32[4,8,64,128]{3,2,1,0:T(8,128)}), f32[4,8,64,128]{3,2,1,0:T(8,128)S(1)}, u32[]{:S(2)}, u32[]{:S(2)}) async-start(f32[4,8,64,128]{3,2,1,0:T(8,128)} %bitcast.13), calls=%async_computation | async-start | bytes 2097152 | tf_op jit(solution)/shard_map/all_to_all | solution.py:58
